TPU v7x, 32 devices: a whole 2x2x4 slice. The times are simulated.
32 devices in a mesh: grp: 2 (over y), lat: 4 (over z), lon: 2 (over x), ch: 2 (over core).
Axes of the slice: x: 2, y: 2, z: 4, core: 2. Of those that a mesh axis runs over, the one named last changes fastest.
Arguments:
- noisy_state: bfloat16 [256, 32, 512], P(('grp', 'ch'), 'lat', 'lon'), parts along dimension 0, may hold values from -6 to 6
- kernel_in: bfloat16 [3, 3, 128, 128], replicated, may hold values from -0.1875 to 0.1875
- bias_in: float32 [128], replicated, may hold values from -4 to 4
- kernel_out: bfloat16 [3, 3, 128, 128], replicated, may hold values from -0.1875 to 0.1875
- interp_weight: bfloat16 [64, 128, 128], P(('grp', 'lat', 'lon')), parts along dimension 0, may hold values from -0.5 to 0.5
- observed: bfloat16 [64, 128, 128], P(('grp', 'lat', 'lon'), 'ch'), parts along dimension 0, may hold values from -6 to 6
- obs_precision: bfloat16 [64, 128], P(('grp', 'lat', 'lon')), parts along dimension 0, may hold values from 0.29882812 to 3
- dest_tile: int32 [64], P(('grp', 'lat', 'lon')), parts along dimension 0, may hold values from 0 to 3, as said below
- row_offset: int32 [64], P(('grp', 'lat', 'lon')), parts along dimension 0, may hold values from 0 to 4
- col_offset: int32 [64], P(('grp', 'lat', 'lon')), parts along dimension 0, may hold values from 0 to 224
Outputs:
- next_state: float32 [256, 32, 512], P(('grp', 'ch'), 'lat', 'lon'), parts along dimension 0
- innovation: bfloat16 [64, 128, 128], P(('grp', 'lat', 'lon'), 'ch'), parts along dimension 0
There are 2 independent parts, one for each index of `grp`. A program takes and returns all parts, laid end to end along the dimension named above; an argument that names none is the same for every part. Nothing has to cross between parts.
Inputs may be any that keep to these rules, and one draw needn't show every extreme that they name: `dest_tile`: the 4 blocks of one device name any one latitude tile at most 2 times; a block's tile lies in the longitude column of the device that holds the block.
All inputs are finite; a program needn't handle non-finite values.
Results may differ from a plain program's by a relative error of at most 0.0085.
Values may be sent and summed in bfloat16 or wider, within the bound.
No kernel may reach another device: no remote copies, remote signals or barrier semaphores. Data moves between devices by JAX's collectives and lax.ppermute only.
A program may use at most 64 MiB of HBM per device.

v0:
```python
import jax
import jax.numpy as jnp
from jax import lax
from jax.sharding import PartitionSpec as P

OBS = 128
PH = 4
PW = 32
CAP = 2
keep_rate = 0.6
blend_rate = 0.4
guide_rate = 0.3


def extended(shard, sides, width):
    for axis, dim in sides:
        size, length = (lax.axis_size(axis), shard.shape[dim])
        up = [(i, (i + 1) % size) for i in range(size)]
        down = [(j, i) for i, j in up]
        last = lax.slice_in_dim(shard, length - width, length, axis=dim)
        initial = lax.slice_in_dim(shard, 0, width, axis=dim)
        before = lax.ppermute(last, axis, up)
        after = lax.ppermute(initial, axis, down)
        shard = jnp.concatenate([before, shard, after], axis=dim)
    return shard


def with_rims(grid_field):
    padded = extended(grid_field, (("lat", 1), ("lon", 2)), 1)
    position = lax.axis_index("lat")
    lat_count = lax.axis_size("lat")
    levels = lax.broadcasted_iota(jnp.int32, (1, padded.shape[1], 1), 1)
    inside = ((levels > 0) | (position > 0)) & (
        (levels < padded.shape[1] - 1) | (position < lat_count - 1)
    )
    return jnp.where(inside, padded, jnp.zeros((), padded.dtype))


def apply_taps(running, kernel_part, padded, grid_rows, grid_cols):
    in_count = padded.shape[0]
    out_count = kernel_part.shape[2]
    for tap_row in range(3):
        stacked = jnp.concatenate(
            [
                padded[:, tap_row : tap_row + grid_rows, tap_col : tap_col + grid_cols]
                for tap_col in range(3)
            ],
            axis=0,
        )
        row_kernel = jnp.transpose(kernel_part[tap_row], (1, 0, 2)).reshape(out_count, 3 * in_count)
        running = running + jnp.einsum(
            "oi,ihw->ohw", row_kernel, stacked, preferred_element_type=jnp.float32
        )
    return running


def convolve(grid_field, kernel_rows):
    padded = with_rims(grid_field)
    grid_rows, grid_cols = (grid_field.shape[1], grid_field.shape[2])
    initial = jnp.zeros((kernel_rows.shape[2], grid_rows, grid_cols), jnp.float32)
    return apply_taps(
        initial, kernel_rows, lax.all_gather(padded, "ch", axis=0, tiled=True), grid_rows, grid_cols
    )


def forward_rows(kernel, first_channel, own_channels):
    return lax.dynamic_slice_in_dim(kernel, first_channel, own_channels, 2)


def adjoint_rows(kernel, first_channel, own_channels):
    columns = lax.dynamic_slice_in_dim(kernel, first_channel, own_channels, 3)
    return jnp.transpose(columns[::-1, ::-1], (0, 1, 3, 2))


def extract(grid_field, patch_rows, patch_cols):

    def take_one(row_start, col_start):
        return lax.dynamic_slice(
            grid_field,
            (jnp.zeros((), jnp.int32), row_start, col_start),
            (grid_field.shape[0], PH, PW),
        )

    return jax.vmap(take_one)(patch_rows, patch_cols)


def spread(grad_patch, patch_rows, patch_cols, grid_shape):
    cell_rows = patch_rows[:, None, None] + lax.broadcasted_iota(jnp.int32, (1, PH, 1), 1)
    cell_cols = patch_cols[:, None, None] + lax.broadcasted_iota(jnp.int32, (1, 1, PW), 2)
    return (
        jnp.zeros(grid_shape, jnp.float32)
        .at[:, cell_rows, cell_cols]
        .add(jnp.moveaxis(grad_patch, 1, 0))
    )


def slot_plan(dest_tile, lat_tiles):
    blocks = dest_tile.shape[0]
    matches = (dest_tile[:, None] == lax.broadcasted_iota(jnp.int32, (1, lat_tiles), 1)).astype(
        jnp.int32
    )
    before = jnp.cumsum(matches, axis=0) - matches
    slot_rank = jnp.sum(before * matches, axis=1)
    flat_slot = dest_tile * CAP + slot_rank
    filler = (
        jnp.full((lat_tiles * CAP,), blocks, jnp.int32)
        .at[flat_slot]
        .set(lax.iota(jnp.int32, blocks))
    )
    filled = filler < blocks
    source = jnp.minimum(filler, blocks - 1)
    return (flat_slot, source, filled)


def observe(denoised, interp_weight, observed, obs_precision, dest_tile, row_offset, col_offset):
    own_channels = denoised.shape[0]
    grid_shape = denoised.shape
    lat_tiles = lax.axis_size("lat")
    slots = lat_tiles * CAP
    flat_slot, source, filled = slot_plan(dest_tile, lat_tiles)
    rows_out = row_offset[source].reshape(lat_tiles, CAP)
    cols_out = col_offset[source].reshape(lat_tiles, CAP)
    weights_out = jnp.where(
        filled[:, None, None], interp_weight[source], jnp.zeros((), jnp.bfloat16)
    ).reshape(lat_tiles, CAP, OBS, PH * PW)
    values_out = observed[source].reshape(lat_tiles, CAP, own_channels, OBS)
    scale_out = jnp.where(
        filled[:, None], obs_precision[source], jnp.zeros((), jnp.bfloat16)
    ).reshape(lat_tiles, CAP, OBS)
    arrived = (
        lax.all_to_all(weights_out, "lat", split_axis=0, concat_axis=0, tiled=True),
        lax.all_to_all(values_out, "lat", split_axis=0, concat_axis=0, tiled=True),
        lax.all_to_all(scale_out, "lat", split_axis=0, concat_axis=0, tiled=True),
        lax.all_to_all(rows_out, "lat", split_axis=0, concat_axis=0, tiled=True),
        lax.all_to_all(cols_out, "lat", split_axis=0, concat_axis=0, tiled=True),
    )
    weights_in = arrived[0].reshape(slots, OBS, PH * PW)
    values_in = arrived[1].reshape(slots, own_channels, OBS)
    scale_in = arrived[2].reshape(slots, OBS)
    rows_in = arrived[3].reshape(slots)
    cols_in = arrived[4].reshape(slots)
    patches = extract(denoised, rows_in, cols_in).reshape(slots, own_channels, PH * PW)
    predicted = jnp.einsum("scp,sop->sco", patches, weights_in, preferred_element_type=jnp.float32)
    residual = predicted - values_in.astype(jnp.float32)
    rounded = residual.astype(jnp.bfloat16).reshape(lat_tiles, CAP, own_channels, OBS)
    returned = lax.all_to_all(rounded, "lat", split_axis=0, concat_axis=0, tiled=True).reshape(
        slots, own_channels, OBS
    )
    innovation = returned[flat_slot]
    weighted = (residual * scale_in.astype(jnp.float32)[:, None, :]).astype(jnp.bfloat16)
    pulled = jnp.einsum("sco,sop->scp", weighted, weights_in, preferred_element_type=jnp.float32)
    grad_field = spread(pulled.reshape(slots, own_channels, PH, PW), rows_in, cols_in, grid_shape)
    return (grad_field, innovation)


def body(
    noisy_state,
    kernel_in,
    bias_in,
    kernel_out,
    interp_weight,
    observed,
    obs_precision,
    dest_tile,
    row_offset,
    col_offset,
):
    own_channels = noisy_state.shape[0]
    first_channel = lax.axis_index("ch") * own_channels
    bias_local = lax.dynamic_slice_in_dim(bias_in, first_channel, own_channels, 0)
    pre_act = (
        convolve(noisy_state, forward_rows(kernel_in, first_channel, own_channels))
        + bias_local[:, None, None]
    )
    hidden = jax.nn.silu(pre_act).astype(jnp.bfloat16)
    denoised = (
        noisy_state.astype(jnp.float32)
        + convolve(hidden, forward_rows(kernel_out, first_channel, own_channels))
    ).astype(jnp.bfloat16)
    grad_field, innovation = observe(
        denoised, interp_weight, observed, obs_precision, dest_tile, row_offset, col_offset
    )
    grad_round = grad_field.astype(jnp.bfloat16)
    back_hidden = convolve(grad_round, adjoint_rows(kernel_out, first_channel, own_channels))
    sigmoid_act = jax.nn.sigmoid(pre_act)
    grad_pre = (back_hidden * sigmoid_act * (1.0 + pre_act * (1.0 - sigmoid_act))).astype(
        jnp.bfloat16
    )
    grad_state = grad_field + convolve(
        grad_pre, adjoint_rows(kernel_in, first_channel, own_channels)
    )
    next_state = (
        keep_rate * noisy_state.astype(jnp.float32)
        + blend_rate * denoised.astype(jnp.float32)
        - guide_rate * grad_state
    )
    return (next_state, innovation)


def solution(mesh):
    return jax.shard_map(
        body,
        mesh=mesh,
        in_specs=(
            P(("grp", "ch"), "lat", "lon"),
            P(),
            P(),
            P(),
            P(("grp", "lat", "lon"), None, None),
            P(("grp", "lat", "lon"), "ch", None),
            P(("grp", "lat", "lon"), None),
            P(("grp", "lat", "lon")),
            P(("grp", "lat", "lon")),
            P(("grp", "lat", "lon")),
        ),
        out_specs=(P(("grp", "ch"), "lat", "lon"), P(("grp", "lat", "lon"), "ch", None)),
        check_vma=False,
    )
```

profile of v0, /device:TPU:0, one launch (start us, length us, event | category | flops | bytes accessed | tf_op | source)
XLA Modules:
  0.0 143.8 jit_solution(14844164952837276044)
XLA Ops:
  0.7 1.2 fusion.163
  1.9 3.1 %collective-permute-start = (bf16[64,1,256]{2,0,1:T(8,128)(2,1)S(1)}, bf16[64,1,256]{2,0,1:T(8,128)(2,1)S(1)}, u32[]{:S(2)}, u32[]{:S(2)}) collective-permute-start(bf16[64,1,256]{2,0,1:T(8,128)(2,1)S(1)} %copy.179), channel_id=1, source_target_pairs={{0,4},{4,8},{8,12},{12,0},{1,5},{5,9},{9,13},{13,1},{2,6},{6,10},{... | collective-permute-start | bytes 98312 | tf_op jit(solution)/shard_map/ppermute | solution.py:22
  5.0 2.1 %collective-permute-start.1 = (bf16[64,1,256]{2,0,1:T(8,128)(2,1)S(1)}, bf16[64,1,256]{2,0,1:T(8,128)(2,1)S(1)}, u32[]{:S(2)}, u32[]{:S(2)}) collective-permute-start(bf16[64,1,256]{2,0,1:T(8,128)(2,1)S(1)} %copy.180), channel_id=1, source_target_pairs={{4,0},{8,4},{12,8},{0,12},{5,1},{9,5},{13,9},{1,13},{6,2},{10,6},{... | collective-permute-start | bytes 98312 | tf_op jit(solution)/shard_map/ppermute | solution.py:23
  7.1 0.7 fusion.134
  7.9 0.8 select_reduce_fusion
  8.7 0.7 compare_select_fusion.5
  10.0 1.3 gather_fusion.1
  11.3 0.7 all_to_all.26
  12.0 3.2 %all-to-all-start.1 = ((s32[4,1,2]{2,1,0:T(1,128)}), s32[4,1,2]{2,1,0:T(1,128)S(1)}, u32[]{:S(2)}, u32[]{:S(2)}) async-start(s32[4,1,2]{2,1,0:T(1,128)} %bitcast.13), calls=%async_computation.1 | async-start | bytes 4096 | tf_op jit(solution)/shard_map/all_to_all | solution.py:135
  16.3 0.6 gather_fusion
  17.0 0.7 all_to_all.24
  18.3 1.2 gather_fusion.3
  20.1 0.8 broadcast_select_fusion
  20.9 0.7 broadcast_select_fusion.2
  21.6 5.1 %all-to-all-start = ((s32[4,1,2]{2,1,0:T(1,128)}), s32[4,1,2]{2,1,0:T(1,128)S(1)}, u32[]{:S(2)}, u32[]{:S(2)}) async-start(s32[4,1,2]{2,1,0:T(1,128)} %bitcast.12), calls=%async_computation | async-start | bytes 4096 | tf_op jit(solution)/shard_map/all_to_all | solution.py:134
  27.2 0.7 reduce.14
  28.0 4.2 %all-to-all-done = s32[4,1,2]{2,1,0:T(1,128)S(1)} async-done(((s32[4,1,2]{2,1,0:T(1,128)}), s32[4,1,2]{2,1,0:T(1,128)S(1)}, u32[]{:S(2)}, u32[]{:S(2)}) %all-to-all-start) | async-done | bytes 64 | tf_op jit(solution)/shard_map/all_to_all | solution.py:134
  32.2 3.2 %all-to-all-start.4 = ((bf16[4,2,128]{2,1,0:T(2,128)(2,1)}), bf16[4,2,128]{2,1,0:T(2,128)(2,1)S(1)}, u32[]{:S(2)}, u32[]{:S(2)}) async-start(bf16[4,2,128]{2,1,0:T(2,128)(2,1)} %broadcast_select_fusion.2), calls=%async_computation.4 | async-start | bytes 4096 | tf_op jit(solution)/shard_map/all_to_all | solution.py:133
  35.4 0.7 reduce.15
  36.7 1.7 %collective-permute-start.2 = (bf16[64,10,1]{2,0,1:T(8,128)(2,1)S(1)}, bf16[64,10,1]{2,0,1:T(8,128)(2,1)S(1)}, u32[]{:S(2)}, u32[]{:S(2)}) collective-permute-start(bf16[64,10,1]{2,0,1:T(8,128)(2,1)S(1)} %get-tuple-element.98), channel_id=1, source_target_pairs={{0,2},{2,0},{1,3},{3,1},{4,6},{6,4},{5,7},{7,5},{8,10},{10,8},{9,1... | collective-permute-start | bytes 3848 | tf_op jit(solution)/shard_map/ppermute | solution.py:22
  38.9 3.5 %collective-permute-done.2 = bf16[64,10,1]{2,0,1:T(8,128)(2,1)S(1)} collective-permute-done((bf16[64,10,1]{2,0,1:T(8,128)(2,1)S(1)}, bf16[64,10,1]{2,0,1:T(8,128)(2,1)S(1)}, u32[]{:S(2)}, u32[]{:S(2)}) %collective-permute-start.2) | collective-permute-done | bytes 1312 | tf_op jit(solution)/shard_map/ppermute | solution.py:22
  42.4 1.8 %collective-permute-done.3 = bf16[64,10,1]{2,0,1:T(8,128)(2,1)S(1)} collective-permute-done((bf16[64,10,1]{2,0,1:T(8,128)(2,1)S(1)}, bf16[64,10,1]{2,0,1:T(8,128)(2,1)S(1)}, u32[]{:S(2)}, u32[]{:S(2)}) %collective-permute-start.3) | collective-permute-done | bytes 1312 | tf_op jit(solution)/shard_map/ppermute | solution.py:23
  44.5 2.5 %all_gather.12 = bf16[128,10,258]{2,0,1:T(8,128)(2,1)S(1)} all-gather(bf16[64,10,258]{2,0,1:T(8,128)(2,1)S(1)} %maximum_select_fusion), channel_id=1, replica_groups=mesh['grp'=2,'lat'=4,'lon'=2,'ch'=2] {'ch'}, dimensions={0}, use_global_device_ids=true | all-gather | bytes 990720 | tf_op jit(solution)/shard_map/all_gather | solution.py:62
  47.0 1.2 fusion.153
  49.0 1.2 multiply_convert_fusion
  50.2 1.7 %collective-permute-start.4 = (bf16[64,1,256]{2,0,1:T(8,128)(2,1)S(1)}, bf16[64,1,256]{2,0,1:T(8,128)(2,1)S(1)}, u32[]{:S(2)}, u32[]{:S(2)}) collective-permute-start(bf16[64,1,256]{2,0,1:T(8,128)(2,1)S(1)} %get-tuple-element.116), channel_id=1, source_target_pairs={{0,4},{4,8},{8,12},{12,0},{1,5},{5,9},{9,13},{13,1},{2,6},{6,10},{... | collective-permute-start | bytes 98312 | tf_op jit(solution)/shard_map/ppermute | solution.py:22
  51.9 2.1 %collective-permute-start.5 = (bf16[64,1,256]{2,0,1:T(8,128)(2,1)S(1)}, bf16[64,1,256]{2,0,1:T(8,128)(2,1)S(1)}, u32[]{:S(2)}, u32[]{:S(2)}) collective-permute-start(bf16[64,1,256]{2,0,1:T(8,128)(2,1)S(1)} %get-tuple-element.117), channel_id=1, source_target_pairs={{4,0},{8,4},{12,8},{0,12},{5,1},{9,5},{13,9},{1,13},{6,2},{10,6},{... | collective-permute-start | bytes 98312 | tf_op jit(solution)/shard_map/ppermute | solution.py:23
  54.1 2.0 %collective-permute-done.4 = bf16[64,1,256]{2,0,1:T(8,128)(2,1)S(1)} collective-permute-done((bf16[64,1,256]{2,0,1:T(8,128)(2,1)S(1)}, bf16[64,1,256]{2,0,1:T(8,128)(2,1)S(1)}, u32[]{:S(2)}, u32[]{:S(2)}) %collective-permute-start.4) | collective-permute-done | bytes 32800 | tf_op jit(solution)/shard_map/ppermute | solution.py:22
  56.4 1.6 %collective-permute-start.6 = (bf16[64,10,1]{2,0,1:T(8,128)(2,1)S(1)}, bf16[64,10,1]{2,0,1:T(8,128)(2,1)S(1)}, u32[]{:S(2)}, u32[]{:S(2)}) collective-permute-start(bf16[64,10,1]{2,0,1:T(8,128)(2,1)S(1)} %get-tuple-element.96), channel_id=1, source_target_pairs={{0,2},{2,0},{1,3},{3,1},{4,6},{6,4},{5,7},{7,5},{8,10},{10,8},{9,1... | collective-permute-start | bytes 3848 | tf_op jit(solution)/shard_map/ppermute | solution.py:22
  58.6 4.8 %all-to-all-start.3 = ((bf16[4,2,64,128]{3,2,1,0:T(8,128)(2,1)}), bf16[4,2,64,128]{3,2,1,0:T(8,128)(2,1)S(1)}, u32[]{:S(2)}, u32[]{:S(2)}) async-start(bf16[4,2,64,128]{3,2,1,0:T(8,128)(2,1)} %bitcast.17), calls=%async_computation.3 | async-start | bytes 262144 | tf_op jit(solution)/shard_map/all_to_all | solution.py:132
  63.4 1.4 collective-permute-done.7
  65.1 2.5 %all_gather.13 = bf16[128,10,258]{2,0,1:T(8,128)(2,1)S(1)} all-gather(bf16[64,10,258]{2,0,1:T(8,128)(2,1)S(1)} %maximum_select_fusion.1), channel_id=1, replica_groups=mesh['grp'=2,'lat'=4,'lon'=2,'ch'=2] {'ch'}, dimensions={0}, use_global_device_ids=true | all-gather | bytes 990720 | tf_op jit(solution)/shard_map/all_gather | solution.py:62
  67.6 1.2 fusion.152
  70.1 4.8 %all-to-all-start.2 = ((bf16[4,2,128,128]{3,2,1,0:T(8,128)(2,1)}), bf16[4,2,128,128]{3,2,1,0:T(8,128)(2,1)S(1)}, u32[]{:S(2)}, u32[]{:S(2)}) async-start(bf16[4,2,128,128]{3,2,1,0:T(8,128)(2,1)} %broadcast_select_fusion), calls=%async_computation.2 | async-start | bytes 524288 | tf_op jit(solution)/shard_map/all_to_all | solution.py:131
  74.9 18.2 %while.1 = (s32[]{:T(128)}, bf16[64,8,256]{2,0,1:T(8,128)(2,1)S(1)}, s32[8,3]{0,1:T(4,128)S(1)}, bf16[8,64,4,32]{1,3,2,0:T(8,128)(2,1)S(1)}, s32[]{:T(128)}) while((s32[]{:T(128)}, bf16[64,8,256]{2,0,1:T(8,128)(2,1)S(1)}, s32[8,3]{0,1:T(4,128)S(1)}, bf16[8,64,4,32]{1,3,2,0:T(8,128)(2,1)S(1)}, s32[]{:T(128)}) %tuple.87), condition=%wide.while_cond, body=%wide.while_body.sunk | while | flops 2 | bytes 163957 | solution.py:78
  75.6 1.4 constant_dynamic-slice_fusion.7
  77.8 1.4 constant_dynamic-slice_fusion.7
  80.1 1.4 constant_dynamic-slice_fusion.7
  82.4 1.4 constant_dynamic-slice_fusion.7
  84.6 1.4 constant_dynamic-slice_fusion.7
  86.9 1.4 constant_dynamic-slice_fusion.7
  89.2 1.4 constant_dynamic-slice_fusion.7
  91.5 1.4 constant_dynamic-slice_fusion.7
  93.1 1.0 fusion.164
  94.3 6.3 %scatter_custom_fusion.1 = f32[64,2048]{0,1:T(8,128)S(1)} fusion(s32[1024]{0:T(1024)S(1)} %reshape.338, f32[1024,64]{1,0:T(8,128)S(1)} %bitcast.128, f32[]{:T(128)} %constant.30.clone.1), kind=kCustom, calls=%fused_computation.104 | custom fusion | flops 65536 | bytes 524292
  101.0 2.1 %collective-permute-start.8 = (bf16[64,1,256]{2,0,1:T(8,128)(2,1)S(1)}, bf16[64,1,256]{2,0,1:T(8,128)(2,1)S(1)}, u32[]{:S(2)}, u32[]{:S(2)}) collective-permute-start(bf16[64,1,256]{2,0,1:T(8,128)(2,1)S(1)} %get-tuple-element.114), channel_id=1, source_target_pairs={{0,4},{4,8},{8,12},{12,0},{1,5},{5,9},{9,13},{13,1},{2,6},{6,10},{... | collective-permute-start | bytes 98312 | tf_op jit(solution)/shard_map/ppermute | solution.py:22
  103.1 2.0 %collective-permute-start.9 = (bf16[64,1,256]{2,0,1:T(8,128)(2,1)S(1)}, bf16[64,1,256]{2,0,1:T(8,128)(2,1)S(1)}, u32[]{:S(2)}, u32[]{:S(2)}) collective-permute-start(bf16[64,1,256]{2,0,1:T(8,128)(2,1)S(1)} %get-tuple-element.115), channel_id=1, source_target_pairs={{4,0},{8,4},{12,8},{0,12},{5,1},{9,5},{13,9},{1,13},{6,2},{10,6},{... | collective-permute-start | bytes 98312 | tf_op jit(solution)/shard_map/ppermute | solution.py:23
  105.1 1.6 %collective-permute-done.8 = bf16[64,1,256]{2,0,1:T(8,128)(2,1)S(1)} collective-permute-done((bf16[64,1,256]{2,0,1:T(8,128)(2,1)S(1)}, bf16[64,1,256]{2,0,1:T(8,128)(2,1)S(1)}, u32[]{:S(2)}, u32[]{:S(2)}) %collective-permute-start.8) | collective-permute-done | bytes 32800 | tf_op jit(solution)/shard_map/ppermute | solution.py:22
  107.3 1.6 %collective-permute-start.10 = (bf16[64,10,1]{2,0,1:T(8,128)(2,1)S(1)}, bf16[64,10,1]{2,0,1:T(8,128)(2,1)S(1)}, u32[]{:S(2)}, u32[]{:S(2)}) collective-permute-start(bf16[64,10,1]{2,0,1:T(8,128)(2,1)S(1)} %get-tuple-element.94), channel_id=1, source_target_pairs={{0,2},{2,0},{1,3},{3,1},{4,6},{6,4},{5,7},{7,5},{8,10},{10,8},{9,1... | collective-permute-start | bytes 3848 | tf_op jit(solution)/shard_map/ppermute | solution.py:22
  109.4 4.2 %collective-permute-done.10 = bf16[64,10,1]{2,0,1:T(8,128)(2,1)S(1)} collective-permute-done((bf16[64,10,1]{2,0,1:T(8,128)(2,1)S(1)}, bf16[64,10,1]{2,0,1:T(8,128)(2,1)S(1)}, u32[]{:S(2)}, u32[]{:S(2)}) %collective-permute-start.10) | collective-permute-done | bytes 1312 | tf_op jit(solution)/shard_map/ppermute | solution.py:22
  113.6 1.8 %collective-permute-done.11 = bf16[64,10,1]{2,0,1:T(8,128)(2,1)S(1)} collective-permute-done((bf16[64,10,1]{2,0,1:T(8,128)(2,1)S(1)}, bf16[64,10,1]{2,0,1:T(8,128)(2,1)S(1)}, u32[]{:S(2)}, u32[]{:S(2)}) %collective-permute-start.11) | collective-permute-done | bytes 1312 | tf_op jit(solution)/shard_map/ppermute | solution.py:23
  115.7 2.5 %all_gather.14 = bf16[128,10,258]{2,0,1:T(8,128)(2,1)S(1)} all-gather(bf16[64,10,258]{2,0,1:T(8,128)(2,1)S(1)} %maximum_select_fusion.2), channel_id=1, replica_groups=mesh['grp'=2,'lat'=4,'lon'=2,'ch'=2] {'ch'}, dimensions={0}, use_global_device_ids=true | all-gather | bytes 990720 | tf_op jit(solution)/shard_map/all_gather | solution.py:62
  118.2 1.2 fusion.151
  120.2 0.6 copy-done.10
  121.3 1.5 %collective-permute-start.12 = (bf16[64,1,256]{2,0,1:T(8,128)(2,1)S(1)}, bf16[64,1,256]{2,0,1:T(8,128)(2,1)S(1)}, u32[]{:S(2)}, u32[]{:S(2)}) collective-permute-start(bf16[64,1,256]{2,0,1:T(8,128)(2,1)S(1)} %get-tuple-element.112), channel_id=1, source_target_pairs={{0,4},{4,8},{8,12},{12,0},{1,5},{5,9},{9,13},{13,1},{2,6},{6,10},{... | collective-permute-start | bytes 98312 | tf_op jit(solution)/shard_map/ppermute | solution.py:22
  122.8 2.4 %collective-permute-start.13 = (bf16[64,1,256]{2,0,1:T(8,128)(2,1)S(1)}, bf16[64,1,256]{2,0,1:T(8,128)(2,1)S(1)}, u32[]{:S(2)}, u32[]{:S(2)}) collective-permute-start(bf16[64,1,256]{2,0,1:T(8,128)(2,1)S(1)} %get-tuple-element.113), channel_id=1, source_target_pairs={{4,0},{8,4},{12,8},{0,12},{5,1},{9,5},{13,9},{1,13},{6,2},{10,6},{... | collective-permute-start | bytes 98312 | tf_op jit(solution)/shard_map/ppermute | solution.py:23
  125.3 1.9 %collective-permute-done.12 = bf16[64,1,256]{2,0,1:T(8,128)(2,1)S(1)} collective-permute-done((bf16[64,1,256]{2,0,1:T(8,128)(2,1)S(1)}, bf16[64,1,256]{2,0,1:T(8,128)(2,1)S(1)}, u32[]{:S(2)}, u32[]{:S(2)}) %collective-permute-start.12) | collective-permute-done | bytes 32800 | tf_op jit(solution)/shard_map/ppermute | solution.py:22
  127.4 1.6 %collective-permute-start.14 = (bf16[64,10,1]{2,0,1:T(8,128)(2,1)S(1)}, bf16[64,10,1]{2,0,1:T(8,128)(2,1)S(1)}, u32[]{:S(2)}, u32[]{:S(2)}) collective-permute-start(bf16[64,10,1]{2,0,1:T(8,128)(2,1)S(1)} %get-tuple-element.92), channel_id=1, source_target_pairs={{0,2},{2,0},{1,3},{3,1},{4,6},{6,4},{5,7},{7,5},{8,10},{10,8},{9,1... | collective-permute-start | bytes 3848 | tf_op jit(solution)/shard_map/ppermute | solution.py:22
  129.5 5.0 %all-to-all-start.5 = ((bf16[4,2,64,128]{3,2,1,0:T(8,128)(2,1)}), bf16[4,2,64,128]{3,2,1,0:T(8,128)(2,1)S(1)}, u32[]{:S(2)}, u32[]{:S(2)}) async-start(bf16[4,2,64,128]{3,2,1,0:T(8,128)(2,1)} %bitcast.51), calls=%async_computation.5 | async-start | bytes 262144 | tf_op jit(solution)/shard_map/all_to_all | solution.py:146
  134.5 1.7 %collective-permute-done.15 = bf16[64,10,1]{2,0,1:T(8,128)(2,1)S(1)} collective-permute-done((bf16[64,10,1]{2,0,1:T(8,128)(2,1)S(1)}, bf16[64,10,1]{2,0,1:T(8,128)(2,1)S(1)}, u32[]{:S(2)}, u32[]{:S(2)}) %collective-permute-start.15) | collective-permute-done | bytes 1312 | tf_op jit(solution)/shard_map/ppermute | solution.py:23
  136.5 2.5 %all_gather.15 = bf16[128,10,258]{2,0,1:T(8,128)(2,1)S(1)} all-gather(bf16[64,10,258]{2,0,1:T(8,128)(2,1)S(1)} %maximum_select_fusion.3), channel_id=1, replica_groups=mesh['grp'=2,'lat'=4,'lon'=2,'ch'=2] {'ch'}, dimensions={0}, use_global_device_ids=true | all-gather | bytes 990720 | tf_op jit(solution)/shard_map/all_gather | solution.py:62
  139.1 1.2 fusion.150
  141.5 1.1 copy.160
  142.7 1.2 gather_fusion.5
  (160 shorter events, 20.7 us)
Async XLA Ops:
  0.6 17.0 %copy-start = (bf16[4,128,128]{2,1,0:T(8,128)(2,1)S(1)}, bf16[4,128,128]{2,1,0:T(8,128)(2,1)}, u32[]{:S(2)}) copy-start(bf16[4,128,128]{2,1,0:T(8,128)(2,1)} %param.14) | copy-start | bytes 393220
  0.6 14.6 %copy-start.3 = (bf16[3,3,128,128]{3,2,1,0:T(8,128)(2,1)S(1)}, bf16[3,3,128,128]{3,2,1,0:T(8,128)(2,1)}, u32[]{:S(2)}) copy-start(bf16[3,3,128,128]{3,2,1,0:T(8,128)(2,1)} %param.11) | copy-start | bytes 884740
  0.7 14.6 %copy-start.2 = (bf16[3,3,128,128]{3,2,1,0:T(8,128)(2,1)S(1)}, bf16[3,3,128,128]{3,2,1,0:T(8,128)(2,1)}, u32[]{:S(2)}) copy-start(bf16[3,3,128,128]{3,2,1,0:T(8,128)(2,1)} %param.13) | copy-start | bytes 884740
  1.9 34.5 %collective-permute-start = (bf16[64,1,256]{2,0,1:T(8,128)(2,1)S(1)}, bf16[64,1,256]{2,0,1:T(8,128)(2,1)S(1)}, u32[]{:S(2)}, u32[]{:S(2)}) collective-permute-start(bf16[64,1,256]{2,0,1:T(8,128)(2,1)S(1)} %copy.179), channel_id=1, source_target_pairs={{0,4},{4,8},{8,12},{12,0},{1,5},{5,9},{9,13},{13,1},{2,6},{6,10},{... | collective-permute-start | bytes 98312 | tf_op jit(solution)/shard_map/ppermute | solution.py:22
  5.0 31.5 %collective-permute-start.1 = (bf16[64,1,256]{2,0,1:T(8,128)(2,1)S(1)}, bf16[64,1,256]{2,0,1:T(8,128)(2,1)S(1)}, u32[]{:S(2)}, u32[]{:S(2)}) collective-permute-start(bf16[64,1,256]{2,0,1:T(8,128)(2,1)S(1)} %copy.180), channel_id=1, source_target_pairs={{4,0},{8,4},{12,8},{0,12},{5,1},{9,5},{13,9},{1,13},{6,2},{10,6},{... | collective-permute-start | bytes 98312 | tf_op jit(solution)/shard_map/ppermute | solution.py:23
  12.0 9.7 %all-to-all-start.1 = ((s32[4,1,2]{2,1,0:T(1,128)}), s32[4,1,2]{2,1,0:T(1,128)S(1)}, u32[]{:S(2)}, u32[]{:S(2)}) async-start(s32[4,1,2]{2,1,0:T(1,128)} %bitcast.13), calls=%async_computation.1 | async-start | bytes 4096 | tf_op jit(solution)/shard_map/all_to_all | solution.py:135
  15.3 0.7 copy-start.9
  15.3 1.0 copy-start.1
  15.7 2.6 %copy-start.6 = (bf16[4,64,128]{2,1,0:T(8,128)(2,1)S(1)}, bf16[4,64,128]{2,1,0:T(8,128)(2,1)}, u32[]{:S(2)}) copy-start(bf16[4,64,128]{2,1,0:T(8,128)(2,1)} %param.15) | copy-start | bytes 196612
  15.8 3.7 %copy-start.5 = (bf16[4,128]{1,0:T(4,128)(2,1)S(1)}, bf16[4,128]{1,0:T(4,128)(2,1)}, u32[]{:S(2)}) copy-start(bf16[4,128]{1,0:T(4,128)(2,1)} %param.16) | copy-start | bytes 3076
  17.0 19.3 %copy-start.8 = (s32[2]{0:T(128)S(1)}, s32[2]{0:T(128)}, u32[]{:S(2)}) copy-start(s32[2]{0:T(128)} %constant.64) | copy-start | bytes 28
  17.0 19.4 %copy-start.7 = (s32[2]{0:T(128)S(1)}, s32[2]{0:T(128)}, u32[]{:S(2)}) copy-start(s32[2]{0:T(128)} %constant.61) | copy-start | bytes 28
  17.6 18.8 %copy-start.4 = (bf16[64,8,256]{2,1,0:T(8,128)(2,1)S(1)}, bf16[64,8,256]{2,1,0:T(8,128)(2,1)}, u32[]{:S(2)}) copy-start(bf16[64,8,256]{2,1,0:T(8,128)(2,1)} %param.10) | copy-start | bytes 786436
  21.6 10.6 %all-to-all-start = ((s32[4,1,2]{2,1,0:T(1,128)}), s32[4,1,2]{2,1,0:T(1,128)S(1)}, u32[]{:S(2)}, u32[]{:S(2)}) async-start(s32[4,1,2]{2,1,0:T(1,128)} %bitcast.12), calls=%async_computation | async-start | bytes 4096 | tf_op jit(solution)/shard_map/all_to_all | solution.py:134
  32.2 26.4 %all-to-all-start.4 = ((bf16[4,2,128]{2,1,0:T(2,128)(2,1)}), bf16[4,2,128]{2,1,0:T(2,128)(2,1)S(1)}, u32[]{:S(2)}, u32[]{:S(2)}) async-start(bf16[4,2,128]{2,1,0:T(2,128)(2,1)} %broadcast_select_fusion.2), calls=%async_computation.4 | async-start | bytes 4096 | tf_op jit(solution)/shard_map/all_to_all | solution.py:133
  36.7 5.7 %collective-permute-start.2 = (bf16[64,10,1]{2,0,1:T(8,128)(2,1)S(1)}, bf16[64,10,1]{2,0,1:T(8,128)(2,1)S(1)}, u32[]{:S(2)}, u32[]{:S(2)}) collective-permute-start(bf16[64,10,1]{2,0,1:T(8,128)(2,1)S(1)} %get-tuple-element.98), channel_id=1, source_target_pairs={{0,2},{2,0},{1,3},{3,1},{4,6},{6,4},{5,7},{7,5},{8,10},{10,8},{9,1... | collective-permute-start | bytes 3848 | tf_op jit(solution)/shard_map/ppermute | solution.py:22
  38.3 5.8 %collective-permute-start.3 = (bf16[64,10,1]{2,0,1:T(8,128)(2,1)S(1)}, bf16[64,10,1]{2,0,1:T(8,128)(2,1)S(1)}, u32[]{:S(2)}, u32[]{:S(2)}) collective-permute-start(bf16[64,10,1]{2,0,1:T(8,128)(2,1)S(1)} %get-tuple-element.99), channel_id=1, source_target_pairs={{2,0},{0,2},{3,1},{1,3},{6,4},{4,6},{7,5},{5,7},{10,8},{8,10},{11,... | collective-permute-start | bytes 3848 | tf_op jit(solution)/shard_map/ppermute | solution.py:23
  50.2 5.8 %collective-permute-start.4 = (bf16[64,1,256]{2,0,1:T(8,128)(2,1)S(1)}, bf16[64,1,256]{2,0,1:T(8,128)(2,1)S(1)}, u32[]{:S(2)}, u32[]{:S(2)}) collective-permute-start(bf16[64,1,256]{2,0,1:T(8,128)(2,1)S(1)} %get-tuple-element.116), channel_id=1, source_target_pairs={{0,4},{4,8},{8,12},{12,0},{1,5},{5,9},{9,13},{13,1},{2,6},{6,10},{... | collective-permute-start | bytes 98312 | tf_op jit(solution)/shard_map/ppermute | solution.py:22
  51.9 4.3 %collective-permute-start.5 = (bf16[64,1,256]{2,0,1:T(8,128)(2,1)S(1)}, bf16[64,1,256]{2,0,1:T(8,128)(2,1)S(1)}, u32[]{:S(2)}, u32[]{:S(2)}) collective-permute-start(bf16[64,1,256]{2,0,1:T(8,128)(2,1)S(1)} %get-tuple-element.117), channel_id=1, source_target_pairs={{4,0},{8,4},{12,8},{0,12},{5,1},{9,5},{13,9},{1,13},{6,2},{10,6},{... | collective-permute-start | bytes 98312 | tf_op jit(solution)/shard_map/ppermute | solution.py:23
  56.4 7.1 %collective-permute-start.6 = (bf16[64,10,1]{2,0,1:T(8,128)(2,1)S(1)}, bf16[64,10,1]{2,0,1:T(8,128)(2,1)S(1)}, u32[]{:S(2)}, u32[]{:S(2)}) collective-permute-start(bf16[64,10,1]{2,0,1:T(8,128)(2,1)S(1)} %get-tuple-element.96), channel_id=1, source_target_pairs={{0,2},{2,0},{1,3},{3,1},{4,6},{6,4},{5,7},{7,5},{8,10},{10,8},{9,1... | collective-permute-start | bytes 3848 | tf_op jit(solution)/shard_map/ppermute | solution.py:22
  58.0 6.8 %collective-permute-start.7 = (bf16[64,10,1]{2,0,1:T(8,128)(2,1)S(1)}, bf16[64,10,1]{2,0,1:T(8,128)(2,1)S(1)}, u32[]{:S(2)}, u32[]{:S(2)}) collective-permute-start(bf16[64,10,1]{2,0,1:T(8,128)(2,1)S(1)} %get-tuple-element.97), channel_id=1, source_target_pairs={{2,0},{0,2},{3,1},{1,3},{6,4},{4,6},{7,5},{5,7},{10,8},{8,10},{11,... | collective-permute-start | bytes 3848 | tf_op jit(solution)/shard_map/ppermute | solution.py:23
  58.6 11.5 %all-to-all-start.3 = ((bf16[4,2,64,128]{3,2,1,0:T(8,128)(2,1)}), bf16[4,2,64,128]{3,2,1,0:T(8,128)(2,1)S(1)}, u32[]{:S(2)}, u32[]{:S(2)}) async-start(bf16[4,2,64,128]{3,2,1,0:T(8,128)(2,1)} %bitcast.17), calls=%async_computation.3 | async-start | bytes 262144 | tf_op jit(solution)/shard_map/all_to_all | solution.py:132
  70.1 23.0 %all-to-all-start.2 = ((bf16[4,2,128,128]{3,2,1,0:T(8,128)(2,1)}), bf16[4,2,128,128]{3,2,1,0:T(8,128)(2,1)S(1)}, u32[]{:S(2)}, u32[]{:S(2)}) async-start(bf16[4,2,128,128]{3,2,1,0:T(8,128)(2,1)} %broadcast_select_fusion), calls=%async_computation.2 | async-start | bytes 524288 | tf_op jit(solution)/shard_map/all_to_all | solution.py:131
  101.0 5.8 %collective-permute-start.8 = (bf16[64,1,256]{2,0,1:T(8,128)(2,1)S(1)}, bf16[64,1,256]{2,0,1:T(8,128)(2,1)S(1)}, u32[]{:S(2)}, u32[]{:S(2)}) collective-permute-start(bf16[64,1,256]{2,0,1:T(8,128)(2,1)S(1)} %get-tuple-element.114), channel_id=1, source_target_pairs={{0,4},{4,8},{8,12},{12,0},{1,5},{5,9},{9,13},{13,1},{2,6},{6,10},{... | collective-permute-start | bytes 98312 | tf_op jit(solution)/shard_map/ppermute | solution.py:22
  103.1 4.0 %collective-permute-start.9 = (bf16[64,1,256]{2,0,1:T(8,128)(2,1)S(1)}, bf16[64,1,256]{2,0,1:T(8,128)(2,1)S(1)}, u32[]{:S(2)}, u32[]{:S(2)}) collective-permute-start(bf16[64,1,256]{2,0,1:T(8,128)(2,1)S(1)} %get-tuple-element.115), channel_id=1, source_target_pairs={{4,0},{8,4},{12,8},{0,12},{5,1},{9,5},{13,9},{1,13},{6,2},{10,6},{... | collective-permute-start | bytes 98312 | tf_op jit(solution)/shard_map/ppermute | solution.py:23
  107.3 6.3 %collective-permute-start.10 = (bf16[64,10,1]{2,0,1:T(8,128)(2,1)S(1)}, bf16[64,10,1]{2,0,1:T(8,128)(2,1)S(1)}, u32[]{:S(2)}, u32[]{:S(2)}) collective-permute-start(bf16[64,10,1]{2,0,1:T(8,128)(2,1)S(1)} %get-tuple-element.94), channel_id=1, source_target_pairs={{0,2},{2,0},{1,3},{3,1},{4,6},{6,4},{5,7},{7,5},{8,10},{10,8},{9,1... | collective-permute-start | bytes 3848 | tf_op jit(solution)/shard_map/ppermute | solution.py:22
  108.9 6.4 %collective-permute-start.11 = (bf16[64,10,1]{2,0,1:T(8,128)(2,1)S(1)}, bf16[64,10,1]{2,0,1:T(8,128)(2,1)S(1)}, u32[]{:S(2)}, u32[]{:S(2)}) collective-permute-start(bf16[64,10,1]{2,0,1:T(8,128)(2,1)S(1)} %get-tuple-element.95), channel_id=1, source_target_pairs={{2,0},{0,2},{3,1},{1,3},{6,4},{4,6},{7,5},{5,7},{10,8},{8,10},{11,... | collective-permute-start | bytes 3848 | tf_op jit(solution)/shard_map/ppermute | solution.py:23
  119.8 1.0 copy-start.10
  121.3 5.8 %collective-permute-start.12 = (bf16[64,1,256]{2,0,1:T(8,128)(2,1)S(1)}, bf16[64,1,256]{2,0,1:T(8,128)(2,1)S(1)}, u32[]{:S(2)}, u32[]{:S(2)}) collective-permute-start(bf16[64,1,256]{2,0,1:T(8,128)(2,1)S(1)} %get-tuple-element.112), channel_id=1, source_target_pairs={{0,4},{4,8},{8,12},{12,0},{1,5},{5,9},{9,13},{13,1},{2,6},{6,10},{... | collective-permute-start | bytes 98312 | tf_op jit(solution)/shard_map/ppermute | solution.py:22
  122.8 4.4 %collective-permute-start.13 = (bf16[64,1,256]{2,0,1:T(8,128)(2,1)S(1)}, bf16[64,1,256]{2,0,1:T(8,128)(2,1)S(1)}, u32[]{:S(2)}, u32[]{:S(2)}) collective-permute-start(bf16[64,1,256]{2,0,1:T(8,128)(2,1)S(1)} %get-tuple-element.113), channel_id=1, source_target_pairs={{4,0},{8,4},{12,8},{0,12},{5,1},{9,5},{13,9},{1,13},{6,2},{10,6},{... | collective-permute-start | bytes 98312 | tf_op jit(solution)/shard_map/ppermute | solution.py:23
  127.4 7.1 %collective-permute-start.14 = (bf16[64,10,1]{2,0,1:T(8,128)(2,1)S(1)}, bf16[64,10,1]{2,0,1:T(8,128)(2,1)S(1)}, u32[]{:S(2)}, u32[]{:S(2)}) collective-permute-start(bf16[64,10,1]{2,0,1:T(8,128)(2,1)S(1)} %get-tuple-element.92), channel_id=1, source_target_pairs={{0,2},{2,0},{1,3},{3,1},{4,6},{6,4},{5,7},{7,5},{8,10},{10,8},{9,1... | collective-permute-start | bytes 3848 | tf_op jit(solution)/shard_map/ppermute | solution.py:22
  129.0 7.2 %collective-permute-start.15 = (bf16[64,10,1]{2,0,1:T(8,128)(2,1)S(1)}, bf16[64,10,1]{2,0,1:T(8,128)(2,1)S(1)}, u32[]{:S(2)}, u32[]{:S(2)}) collective-permute-start(bf16[64,10,1]{2,0,1:T(8,128)(2,1)S(1)} %get-tuple-element.93), channel_id=1, source_target_pairs={{2,0},{0,2},{3,1},{1,3},{6,4},{4,6},{7,5},{5,7},{10,8},{8,10},{11,... | collective-permute-start | bytes 3848 | tf_op jit(solution)/shard_map/ppermute | solution.py:23
  129.5 13.2 %all-to-all-start.5 = ((bf16[4,2,64,128]{3,2,1,0:T(8,128)(2,1)}), bf16[4,2,64,128]{3,2,1,0:T(8,128)(2,1)S(1)}, u32[]{:S(2)}, u32[]{:S(2)}) async-start(bf16[4,2,64,128]{3,2,1,0:T(8,128)(2,1)} %bitcast.51), calls=%async_computation.5 | async-start | bytes 262144 | tf_op jit(solution)/shard_map/all_to_all | solution.py:146
where the time goes:
time: 145 us; the launch traced here: 144 us
  starting transfers between devices  51.6 us (36%)
  local copies, waits for them, and re-layouts  35.9 us (25%)
  waiting for transfers between devices  24.5 us (17%)
  other arithmetic  13.2 us (9%)
  blocking collectives  10 us (7%)
  matrix products  7.13 us (5%)
    gather x48, local copies, waits for them, and re-layouts  17.9 us
    ppermute x8, starting transfers between devices, extended(): before = lax.ppermute(last, axis, up)  14.8 us
    ppermute x8, waiting for transfers between devices, extended(): before = lax.ppermute(last, axis, up)  13.1 us
    ppermute x8, starting transfers between devices, extended(): after = lax.ppermute(initial, axis, down)  10.6 us
    all_gather x4, blocking collectives, convolve(): lax.all_gather(padded, 'ch', axis=0, tiled=True)  10 us
    ppermute x8, waiting for transfers between devices, extended(): after = lax.ppermute(initial, axis, down)  7.17 us
    unnamed x5, other arithmetic  6.44 us
    dot_general x12, matrix products, apply_taps(): jnp.einsum('oi,ihw->ohw', row_kernel, stacked, preferred_element_type=jnp...  5.9 us
  transfers between devices with their start and end apart: 22, of which 13 were waited for; matrix products, arithmetic and copies ran while one was open for 28% of the time, Pallas kernels for 0%

commit v1 on v0

--- a/solution.py
+++ b/solution.py
@@ -10,6 +10,29 @@
 keep_rate = 0.6
 blend_rate = 0.4
 guide_rate = 0.3
+
+
+def in_blocks(shard, dim, size):
+    shape = shard.shape
+    blocks = shard.reshape(*shape[:dim], size, shape[dim] // size, *shape[dim + 1 :])
+    return jnp.moveaxis(blocks, dim, 0)
+
+
+def joined_along(blocks, dim):
+    shape = list(blocks.shape[1:])
+    shape[dim] *= blocks.shape[0]
+    return jnp.moveaxis(blocks, 0, dim).reshape(shape)
+
+
+def pairwise_exchange(x, axis, split_dim, concat_dim):
+    peers, index = (lax.axis_size(axis), lax.axis_index(axis))
+    blocks = in_blocks(x, split_dim, peers)
+    gathered = [blocks[index]]
+    for step in range(1, peers):
+        sent = blocks[index ^ step]
+        gathered.append(lax.ppermute(sent, axis, [(i, i ^ step) for i in range(peers)]))
+    blocks = jnp.stack(gathered)[index ^ jnp.arange(peers)]
+    return joined_along(blocks, concat_dim)
 
 
 def extended(shard, sides, width):
@@ -131,7 +154,7 @@
         lax.all_to_all(weights_out, "lat", split_axis=0, concat_axis=0, tiled=True),
         lax.all_to_all(values_out, "lat", split_axis=0, concat_axis=0, tiled=True),
         lax.all_to_all(scale_out, "lat", split_axis=0, concat_axis=0, tiled=True),
-        lax.all_to_all(rows_out, "lat", split_axis=0, concat_axis=0, tiled=True),
+        pairwise_exchange(rows_out, "lat", 0, 0),
         lax.all_to_all(cols_out, "lat", split_axis=0, concat_axis=0, tiled=True),
     )
     weights_in = arrived[0].reshape(slots, OBS, PH * PW)

time: 145 us -> 142 us (0.979)
  waiting for transfers between devices: 24.5 us -> 20.8 us
    all_to_all x1 -> x0, starting transfers between devices: 5.06 us -> none  [observe(): lax.all_to_all(rows_out, 'lat', split_axis=0, concat_axis=0, tiled=True)]
    ppermute x0 -> x3, starting transfers between devices: none -> 4.44 us  [pairwise_exchange(): lax.ppermute(sent, axis, [(i, i ^ step) for i in range(peers)])]
    all_to_all x1 -> x0, waiting for transfers between devices: 4.16 us -> none  [observe(): lax.all_to_all(rows_out, 'lat', split_axis=0, concat_axis=0, tiled=True)]
    all_to_all x1, starting transfers between devices: 3.24 us -> 5.06 us  [observe(): lax.all_to_all(scale_out, 'lat', split_axis=0, concat_axis=0, tiled=True)]
    gather x48 -> x49, local copies, waits for them, and re-layouts: 17.9 us -> 18.5 us
  transfers between devices with their start and end apart: 22 -> 24, of which waited for: 13 -> 12; matrix products, arithmetic and copies ran while one was open for 28% -> 29% of each run, Pallas kernels for 0% -> 0%
where the time goes in v1:
time: 142 us; the launch traced here: 141 us
  starting transfers between devices  52.8 us (37%)
  local copies, waits for them, and re-layouts  35.9 us (25%)
  waiting for transfers between devices  20.8 us (15%)
  other arithmetic  12.5 us (9%)
  blocking collectives  10 us (7%)
  matrix products  7.12 us (5%)
    gather x48, local copies, waits for them, and re-layouts  17.9 us
    ppermute x8, starting transfers between devices, extended(): before = lax.ppermute(last, axis, up)  14.7 us
    ppermute x8, waiting for transfers between devices, extended(): before = lax.ppermute(last, axis, up)  13.5 us
    ppermute x8, starting transfers between devices, extended(): after = lax.ppermute(initial, axis, down)  10.7 us
    all_gather x4, blocking collectives, convolve(): lax.all_gather(padded, 'ch', axis=0, tiled=True)  10 us
    ppermute x8, waiting for transfers between devices, extended(): after = lax.ppermute(initial, axis, down)  7.23 us
    unnamed x5, other arithmetic  6.44 us
    dot_general x12, matrix products, apply_taps(): jnp.einsum('oi,ihw->ohw', row_kernel, stacked, preferred_element_type=jnp...  5.89 us
  transfers between devices with their start and end apart: 24, of which 12 were waited for; matrix products, arithmetic and copies ran while one was open for 29% of the time, Pallas kernels for 0%

profile of v1, /device:TPU:0, one launch (start us, length us, event | category | flops | bytes accessed | tf_op | source)
XLA Modules:
  0.0 140.8 jit_solution(1604121698799299416)
XLA Ops:
  0.7 1.2 fusion.167
  1.9 3.1 %collective-permute-start = (bf16[64,1,256]{2,0,1:T(8,128)(2,1)S(1)}, bf16[64,1,256]{2,0,1:T(8,128)(2,1)S(1)}, u32[]{:S(2)}, u32[]{:S(2)}) collective-permute-start(bf16[64,1,256]{2,0,1:T(8,128)(2,1)S(1)} %copy.206), channel_id=1, source_target_pairs={{0,4},{4,8},{8,12},{12,0},{1,5},{5,9},{9,13},{13,1},{2,6},{6,10},{... | collective-permute-start | bytes 98312 | tf_op jit(solution)/shard_map/ppermute | solution.py:45
  5.0 2.1 %collective-permute-start.1 = (bf16[64,1,256]{2,0,1:T(8,128)(2,1)S(1)}, bf16[64,1,256]{2,0,1:T(8,128)(2,1)S(1)}, u32[]{:S(2)}, u32[]{:S(2)}) collective-permute-start(bf16[64,1,256]{2,0,1:T(8,128)(2,1)S(1)} %copy.207), channel_id=1, source_target_pairs={{4,0},{8,4},{12,8},{0,12},{5,1},{9,5},{13,9},{1,13},{6,2},{10,6},{... | collective-permute-start | bytes 98312 | tf_op jit(solution)/shard_map/ppermute | solution.py:46
  7.1 0.7 fusion.134
  7.9 0.8 select_reduce_fusion
  8.7 0.7 compare_select_fusion.6
  10.0 1.3 gather_fusion
  11.5 2.5 %collective-permute-start.9 = (s32[1,2]{1,0:T(1,128)S(1)}, s32[1,2]{1,0:T(1,128)S(1)}, u32[]{:S(2)}, u32[]{:S(2)}) collective-permute-start(s32[1,2]{1,0:T(1,128)S(1)} %get-tuple-element.122), channel_id=1, source_target_pairs={{0,8},{4,12},{8,0},{12,4},{1,9},{5,13},{9,1},{13,5},{2,10},{6,14},... | collective-permute-start | bytes 32 | tf_op jit(solution)/shard_map/ppermute | solution.py:33
  14.0 1.9 %collective-permute-start.10 = (s32[1,2]{1,0:T(1,128)S(1)}, s32[1,2]{1,0:T(1,128)S(1)}, u32[]{:S(2)}, u32[]{:S(2)}) collective-permute-start(s32[1,2]{1,0:T(1,128)S(1)} %get-tuple-element.121), channel_id=1, source_target_pairs={{0,12},{4,8},{8,4},{12,0},{1,13},{5,9},{9,5},{13,1},{2,14},{6,10},... | collective-permute-start | bytes 32 | tf_op jit(solution)/shard_map/ppermute | solution.py:33
  15.9 0.6 gather_fusion.2
  16.5 0.7 all_to_all.18
  17.2 3.2 %all-to-all-start = ((s32[4,1,2]{2,1,0:T(1,128)}), s32[4,1,2]{2,1,0:T(1,128)S(1)}, u32[]{:S(2)}, u32[]{:S(2)}) async-start(s32[4,1,2]{2,1,0:T(1,128)} %bitcast.23), calls=%async_computation | async-start | bytes 4096 | tf_op jit(solution)/shard_map/all_to_all | solution.py:158
  21.6 0.6 gather_fusion.3
  22.3 1.2 gather_fusion.4
  24.1 0.8 broadcast_select_fusion
  24.9 0.7 broadcast_select_fusion.2
  26.4 5.1 %all-to-all-start.3 = ((bf16[4,2,128]{2,1,0:T(2,128)(2,1)}), bf16[4,2,128]{2,1,0:T(2,128)(2,1)S(1)}, u32[]{:S(2)}, u32[]{:S(2)}) async-start(bf16[4,2,128]{2,1,0:T(2,128)(2,1)} %broadcast_select_fusion.2), calls=%async_computation.3 | async-start | bytes 4096 | tf_op jit(solution)/shard_map/all_to_all | solution.py:156
  31.9 0.7 reduce.9
  33.2 1.7 %collective-permute-start.2 = (bf16[64,10,1]{2,0,1:T(8,128)(2,1)S(1)}, bf16[64,10,1]{2,0,1:T(8,128)(2,1)S(1)}, u32[]{:S(2)}, u32[]{:S(2)}) collective-permute-start(bf16[64,10,1]{2,0,1:T(8,128)(2,1)S(1)} %get-tuple-element.98), channel_id=1, source_target_pairs={{0,2},{2,0},{1,3},{3,1},{4,6},{6,4},{5,7},{7,5},{8,10},{10,8},{9,1... | collective-permute-start | bytes 3848 | tf_op jit(solution)/shard_map/ppermute | solution.py:45
  35.4 3.9 %collective-permute-done.2 = bf16[64,10,1]{2,0,1:T(8,128)(2,1)S(1)} collective-permute-done((bf16[64,10,1]{2,0,1:T(8,128)(2,1)S(1)}, bf16[64,10,1]{2,0,1:T(8,128)(2,1)S(1)}, u32[]{:S(2)}, u32[]{:S(2)}) %collective-permute-start.2) | collective-permute-done | bytes 1312 | tf_op jit(solution)/shard_map/ppermute | solution.py:45
  39.3 1.8 %collective-permute-done.3 = bf16[64,10,1]{2,0,1:T(8,128)(2,1)S(1)} collective-permute-done((bf16[64,10,1]{2,0,1:T(8,128)(2,1)S(1)}, bf16[64,10,1]{2,0,1:T(8,128)(2,1)S(1)}, u32[]{:S(2)}, u32[]{:S(2)}) %collective-permute-start.3) | collective-permute-done | bytes 1312 | tf_op jit(solution)/shard_map/ppermute | solution.py:46
  41.4 2.5 %all_gather.12 = bf16[128,10,258]{2,0,1:T(8,128)(2,1)S(1)} all-gather(bf16[64,10,258]{2,0,1:T(8,128)(2,1)S(1)} %maximum_select_fusion), channel_id=1, replica_groups=mesh['grp'=2,'lat'=4,'lon'=2,'ch'=2] {'ch'}, dimensions={0}, use_global_device_ids=true | all-gather | bytes 990720 | tf_op jit(solution)/shard_map/all_gather | solution.py:85
  43.9 1.2 fusion.157
  45.9 1.2 multiply_convert_fusion
  47.1 1.7 %collective-permute-start.4 = (bf16[64,1,256]{2,0,1:T(8,128)(2,1)S(1)}, bf16[64,1,256]{2,0,1:T(8,128)(2,1)S(1)}, u32[]{:S(2)}, u32[]{:S(2)}) collective-permute-start(bf16[64,1,256]{2,0,1:T(8,128)(2,1)S(1)} %get-tuple-element.116), channel_id=1, source_target_pairs={{0,4},{4,8},{8,12},{12,0},{1,5},{5,9},{9,13},{13,1},{2,6},{6,10},{... | collective-permute-start | bytes 98312 | tf_op jit(solution)/shard_map/ppermute | solution.py:45
  48.8 2.1 %collective-permute-start.5 = (bf16[64,1,256]{2,0,1:T(8,128)(2,1)S(1)}, bf16[64,1,256]{2,0,1:T(8,128)(2,1)S(1)}, u32[]{:S(2)}, u32[]{:S(2)}) collective-permute-start(bf16[64,1,256]{2,0,1:T(8,128)(2,1)S(1)} %get-tuple-element.117), channel_id=1, source_target_pairs={{4,0},{8,4},{12,8},{0,12},{5,1},{9,5},{13,9},{1,13},{6,2},{10,6},{... | collective-permute-start | bytes 98312 | tf_op jit(solution)/shard_map/ppermute | solution.py:46
  50.9 2.0 %collective-permute-done.4 = bf16[64,1,256]{2,0,1:T(8,128)(2,1)S(1)} collective-permute-done((bf16[64,1,256]{2,0,1:T(8,128)(2,1)S(1)}, bf16[64,1,256]{2,0,1:T(8,128)(2,1)S(1)}, u32[]{:S(2)}, u32[]{:S(2)}) %collective-permute-start.4) | collective-permute-done | bytes 32800 | tf_op jit(solution)/shard_map/ppermute | solution.py:45
  53.3 1.6 %collective-permute-start.6 = (bf16[64,10,1]{2,0,1:T(8,128)(2,1)S(1)}, bf16[64,10,1]{2,0,1:T(8,128)(2,1)S(1)}, u32[]{:S(2)}, u32[]{:S(2)}) collective-permute-start(bf16[64,10,1]{2,0,1:T(8,128)(2,1)S(1)} %get-tuple-element.96), channel_id=1, source_target_pairs={{0,2},{2,0},{1,3},{3,1},{4,6},{6,4},{5,7},{7,5},{8,10},{10,8},{9,1... | collective-permute-start | bytes 3848 | tf_op jit(solution)/shard_map/ppermute | solution.py:45
  55.5 4.8 %all-to-all-start.2 = ((bf16[4,2,64,128]{3,2,1,0:T(8,128)(2,1)}), bf16[4,2,64,128]{3,2,1,0:T(8,128)(2,1)S(1)}, u32[]{:S(2)}, u32[]{:S(2)}) async-start(bf16[4,2,64,128]{3,2,1,0:T(8,128)(2,1)} %bitcast.27), calls=%async_computation.2 | async-start | bytes 262144 | tf_op jit(solution)/shard_map/all_to_all | solution.py:155
  60.3 1.4 collective-permute-done.7
  62.0 2.5 %all_gather.13 = bf16[128,10,258]{2,0,1:T(8,128)(2,1)S(1)} all-gather(bf16[64,10,258]{2,0,1:T(8,128)(2,1)S(1)} %maximum_select_fusion.1), channel_id=1, replica_groups=mesh['grp'=2,'lat'=4,'lon'=2,'ch'=2] {'ch'}, dimensions={0}, use_global_device_ids=true | all-gather | bytes 990720 | tf_op jit(solution)/shard_map/all_gather | solution.py:85
  64.5 1.2 fusion.156
  66.9 4.9 %all-to-all-start.1 = ((bf16[4,2,128,128]{3,2,1,0:T(8,128)(2,1)}), bf16[4,2,128,128]{3,2,1,0:T(8,128)(2,1)S(1)}, u32[]{:S(2)}, u32[]{:S(2)}) async-start(bf16[4,2,128,128]{3,2,1,0:T(8,128)(2,1)} %broadcast_select_fusion), calls=%async_computation.1 | async-start | bytes 524288 | tf_op jit(solution)/shard_map/all_to_all | solution.py:154
  71.8 18.2 %while.1 = (s32[]{:T(128)}, bf16[64,8,256]{2,0,1:T(8,128)(2,1)S(1)}, s32[8,3]{0,1:T(4,128)S(1)}, bf16[8,64,4,32]{1,3,2,0:T(8,128)(2,1)S(1)}, s32[]{:T(128)}) while((s32[]{:T(128)}, bf16[64,8,256]{2,0,1:T(8,128)(2,1)S(1)}, s32[8,3]{0,1:T(4,128)S(1)}, bf16[8,64,4,32]{1,3,2,0:T(8,128)(2,1)S(1)}, s32[]{:T(128)}) %tuple.90), condition=%wide.while_cond, body=%wide.while_body.sunk | while | flops 2 | bytes 163957 | solution.py:101
  72.5 1.4 %constant_dynamic-slice_fusion.11 = bf16[64,4,32]{2,0,1:T(8,128)(2,1)S(1)} fusion(bf16[64,8,256]{2,0,1:T(8,128)(2,1)S(1)} %get-tuple-element.172, s32[]{:T(128)} %bitcast.137, s32[]{:T(128)} %bitcast.138), kind=kLoop, calls=%fused_computation.11.clone.1 | loop fusion | bytes 32776 | tf_op jit(solution)/shard_map/vmap()/gather
  74.7 1.4 %constant_dynamic-slice_fusion.11 = bf16[64,4,32]{2,0,1:T(8,128)(2,1)S(1)} fusion(bf16[64,8,256]{2,0,1:T(8,128)(2,1)S(1)} %get-tuple-element.172, s32[]{:T(128)} %bitcast.137, s32[]{:T(128)} %bitcast.138), kind=kLoop, calls=%fused_computation.11.clone.1 | loop fusion | bytes 32776 | tf_op jit(solution)/shard_map/vmap()/gather
  76.4 0.6 fusion.185
  77.0 1.4 %constant_dynamic-slice_fusion.11 = bf16[64,4,32]{2,0,1:T(8,128)(2,1)S(1)} fusion(bf16[64,8,256]{2,0,1:T(8,128)(2,1)S(1)} %get-tuple-element.172, s32[]{:T(128)} %bitcast.137, s32[]{:T(128)} %bitcast.138), kind=kLoop, calls=%fused_computation.11.clone.1 | loop fusion | bytes 32776 | tf_op jit(solution)/shard_map/vmap()/gather
  79.3 1.4 %constant_dynamic-slice_fusion.11 = bf16[64,4,32]{2,0,1:T(8,128)(2,1)S(1)} fusion(bf16[64,8,256]{2,0,1:T(8,128)(2,1)S(1)} %get-tuple-element.172, s32[]{:T(128)} %bitcast.137, s32[]{:T(128)} %bitcast.138), kind=kLoop, calls=%fused_computation.11.clone.1 | loop fusion | bytes 32776 | tf_op jit(solution)/shard_map/vmap()/gather
  81.6 1.4 %constant_dynamic-slice_fusion.11 = bf16[64,4,32]{2,0,1:T(8,128)(2,1)S(1)} fusion(bf16[64,8,256]{2,0,1:T(8,128)(2,1)S(1)} %get-tuple-element.172, s32[]{:T(128)} %bitcast.137, s32[]{:T(128)} %bitcast.138), kind=kLoop, calls=%fused_computation.11.clone.1 | loop fusion | bytes 32776 | tf_op jit(solution)/shard_map/vmap()/gather
  83.8 1.4 %constant_dynamic-slice_fusion.11 = bf16[64,4,32]{2,0,1:T(8,128)(2,1)S(1)} fusion(bf16[64,8,256]{2,0,1:T(8,128)(2,1)S(1)} %get-tuple-element.172, s32[]{:T(128)} %bitcast.137, s32[]{:T(128)} %bitcast.138), kind=kLoop, calls=%fused_computation.11.clone.1 | loop fusion | bytes 32776 | tf_op jit(solution)/shard_map/vmap()/gather
  86.1 1.4 %constant_dynamic-slice_fusion.11 = bf16[64,4,32]{2,0,1:T(8,128)(2,1)S(1)} fusion(bf16[64,8,256]{2,0,1:T(8,128)(2,1)S(1)} %get-tuple-element.172, s32[]{:T(128)} %bitcast.137, s32[]{:T(128)} %bitcast.138), kind=kLoop, calls=%fused_computation.11.clone.1 | loop fusion | bytes 32776 | tf_op jit(solution)/shard_map/vmap()/gather
  88.4 1.4 %constant_dynamic-slice_fusion.11 = bf16[64,4,32]{2,0,1:T(8,128)(2,1)S(1)} fusion(bf16[64,8,256]{2,0,1:T(8,128)(2,1)S(1)} %get-tuple-element.172, s32[]{:T(128)} %bitcast.137, s32[]{:T(128)} %bitcast.138), kind=kLoop, calls=%fused_computation.11.clone.1 | loop fusion | bytes 32776 | tf_op jit(solution)/shard_map/vmap()/gather
  90.0 1.0 fusion.168
  91.2 6.3 %scatter_custom_fusion.1 = f32[64,2048]{0,1:T(8,128)S(1)} fusion(s32[1024]{0:T(1024)S(1)} %reshape.354, f32[1024,64]{1,0:T(8,128)S(1)} %bitcast.145, f32[]{:T(128)} %constant.31.clone.1), kind=kCustom, calls=%fused_computation.105 | custom fusion | flops 65536 | bytes 524292
  97.9 2.1 %collective-permute-start.11 = (bf16[64,1,256]{2,0,1:T(8,128)(2,1)S(1)}, bf16[64,1,256]{2,0,1:T(8,128)(2,1)S(1)}, u32[]{:S(2)}, u32[]{:S(2)}) collective-permute-start(bf16[64,1,256]{2,0,1:T(8,128)(2,1)S(1)} %get-tuple-element.114), channel_id=1, source_target_pairs={{0,4},{4,8},{8,12},{12,0},{1,5},{5,9},{9,13},{13,1},{2,6},{6,10},{... | collective-permute-start | bytes 98312 | tf_op jit(solution)/shard_map/ppermute | solution.py:45
  100.0 2.0 %collective-permute-start.12 = (bf16[64,1,256]{2,0,1:T(8,128)(2,1)S(1)}, bf16[64,1,256]{2,0,1:T(8,128)(2,1)S(1)}, u32[]{:S(2)}, u32[]{:S(2)}) collective-permute-start(bf16[64,1,256]{2,0,1:T(8,128)(2,1)S(1)} %get-tuple-element.115), channel_id=1, source_target_pairs={{4,0},{8,4},{12,8},{0,12},{5,1},{9,5},{13,9},{1,13},{6,2},{10,6},{... | collective-permute-start | bytes 98312 | tf_op jit(solution)/shard_map/ppermute | solution.py:46
  102.0 1.6 %collective-permute-done.11 = bf16[64,1,256]{2,0,1:T(8,128)(2,1)S(1)} collective-permute-done((bf16[64,1,256]{2,0,1:T(8,128)(2,1)S(1)}, bf16[64,1,256]{2,0,1:T(8,128)(2,1)S(1)}, u32[]{:S(2)}, u32[]{:S(2)}) %collective-permute-start.11) | collective-permute-done | bytes 32800 | tf_op jit(solution)/shard_map/ppermute | solution.py:45
  104.2 1.6 %collective-permute-start.13 = (bf16[64,10,1]{2,0,1:T(8,128)(2,1)S(1)}, bf16[64,10,1]{2,0,1:T(8,128)(2,1)S(1)}, u32[]{:S(2)}, u32[]{:S(2)}) collective-permute-start(bf16[64,10,1]{2,0,1:T(8,128)(2,1)S(1)} %get-tuple-element.94), channel_id=1, source_target_pairs={{0,2},{2,0},{1,3},{3,1},{4,6},{6,4},{5,7},{7,5},{8,10},{10,8},{9,1... | collective-permute-start | bytes 3848 | tf_op jit(solution)/shard_map/ppermute | solution.py:45
  106.3 4.2 %collective-permute-done.13 = bf16[64,10,1]{2,0,1:T(8,128)(2,1)S(1)} collective-permute-done((bf16[64,10,1]{2,0,1:T(8,128)(2,1)S(1)}, bf16[64,10,1]{2,0,1:T(8,128)(2,1)S(1)}, u32[]{:S(2)}, u32[]{:S(2)}) %collective-permute-start.13) | collective-permute-done | bytes 1312 | tf_op jit(solution)/shard_map/ppermute | solution.py:45
  110.5 1.8 %collective-permute-done.14 = bf16[64,10,1]{2,0,1:T(8,128)(2,1)S(1)} collective-permute-done((bf16[64,10,1]{2,0,1:T(8,128)(2,1)S(1)}, bf16[64,10,1]{2,0,1:T(8,128)(2,1)S(1)}, u32[]{:S(2)}, u32[]{:S(2)}) %collective-permute-start.14) | collective-permute-done | bytes 1312 | tf_op jit(solution)/shard_map/ppermute | solution.py:46
  112.6 2.5 %all_gather.14 = bf16[128,10,258]{2,0,1:T(8,128)(2,1)S(1)} all-gather(bf16[64,10,258]{2,0,1:T(8,128)(2,1)S(1)} %maximum_select_fusion.2), channel_id=1, replica_groups=mesh['grp'=2,'lat'=4,'lon'=2,'ch'=2] {'ch'}, dimensions={0}, use_global_device_ids=true | all-gather | bytes 990720 | tf_op jit(solution)/shard_map/all_gather | solution.py:85
  115.1 1.2 fusion.155
  117.1 0.6 copy-done.10
  118.3 1.5 %collective-permute-start.15 = (bf16[64,1,256]{2,0,1:T(8,128)(2,1)S(1)}, bf16[64,1,256]{2,0,1:T(8,128)(2,1)S(1)}, u32[]{:S(2)}, u32[]{:S(2)}) collective-permute-start(bf16[64,1,256]{2,0,1:T(8,128)(2,1)S(1)} %get-tuple-element.112), channel_id=1, source_target_pairs={{0,4},{4,8},{8,12},{12,0},{1,5},{5,9},{9,13},{13,1},{2,6},{6,10},{... | collective-permute-start | bytes 98312 | tf_op jit(solution)/shard_map/ppermute | solution.py:45
  119.7 2.4 %collective-permute-start.16 = (bf16[64,1,256]{2,0,1:T(8,128)(2,1)S(1)}, bf16[64,1,256]{2,0,1:T(8,128)(2,1)S(1)}, u32[]{:S(2)}, u32[]{:S(2)}) collective-permute-start(bf16[64,1,256]{2,0,1:T(8,128)(2,1)S(1)} %get-tuple-element.113), channel_id=1, source_target_pairs={{4,0},{8,4},{12,8},{0,12},{5,1},{9,5},{13,9},{1,13},{6,2},{10,6},{... | collective-permute-start | bytes 98312 | tf_op jit(solution)/shard_map/ppermute | solution.py:46
  122.2 1.9 %collective-permute-done.15 = bf16[64,1,256]{2,0,1:T(8,128)(2,1)S(1)} collective-permute-done((bf16[64,1,256]{2,0,1:T(8,128)(2,1)S(1)}, bf16[64,1,256]{2,0,1:T(8,128)(2,1)S(1)}, u32[]{:S(2)}, u32[]{:S(2)}) %collective-permute-start.15) | collective-permute-done | bytes 32800 | tf_op jit(solution)/shard_map/ppermute | solution.py:45
  124.3 1.6 %collective-permute-start.17 = (bf16[64,10,1]{2,0,1:T(8,128)(2,1)S(1)}, bf16[64,10,1]{2,0,1:T(8,128)(2,1)S(1)}, u32[]{:S(2)}, u32[]{:S(2)}) collective-permute-start(bf16[64,10,1]{2,0,1:T(8,128)(2,1)S(1)} %get-tuple-element.92), channel_id=1, source_target_pairs={{0,2},{2,0},{1,3},{3,1},{4,6},{6,4},{5,7},{7,5},{8,10},{10,8},{9,1... | collective-permute-start | bytes 3848 | tf_op jit(solution)/shard_map/ppermute | solution.py:45
  126.4 5.0 %all-to-all-start.4 = ((bf16[4,2,64,128]{3,2,1,0:T(8,128)(2,1)}), bf16[4,2,64,128]{3,2,1,0:T(8,128)(2,1)S(1)}, u32[]{:S(2)}, u32[]{:S(2)}) async-start(bf16[4,2,64,128]{3,2,1,0:T(8,128)(2,1)} %bitcast.61), calls=%async_computation.4 | async-start | bytes 262144 | tf_op jit(solution)/shard_map/all_to_all | solution.py:169
  131.4 1.7 %collective-permute-done.18 = bf16[64,10,1]{2,0,1:T(8,128)(2,1)S(1)} collective-permute-done((bf16[64,10,1]{2,0,1:T(8,128)(2,1)S(1)}, bf16[64,10,1]{2,0,1:T(8,128)(2,1)S(1)}, u32[]{:S(2)}, u32[]{:S(2)}) %collective-permute-start.18) | collective-permute-done | bytes 1312 | tf_op jit(solution)/shard_map/ppermute | solution.py:46
  133.5 2.5 %all_gather.15 = bf16[128,10,258]{2,0,1:T(8,128)(2,1)S(1)} all-gather(bf16[64,10,258]{2,0,1:T(8,128)(2,1)S(1)} %maximum_select_fusion.3), channel_id=1, replica_groups=mesh['grp'=2,'lat'=4,'lon'=2,'ch'=2] {'ch'}, dimensions={0}, use_global_device_ids=true | all-gather | bytes 990720 | tf_op jit(solution)/shard_map/all_gather | solution.py:85
  136.0 1.2 fusion.154
  138.5 1.1 copy.186
  139.6 1.2 gather_fusion.6
  (168 shorter events, 20.5 us)
Async XLA Ops:
  0.6 20.9 %copy-start = (bf16[4,128,128]{2,1,0:T(8,128)(2,1)S(1)}, bf16[4,128,128]{2,1,0:T(8,128)(2,1)}, u32[]{:S(2)}) copy-start(bf16[4,128,128]{2,1,0:T(8,128)(2,1)} %param.14) | copy-start | bytes 393220
  0.6 15.2 %copy-start.1 = (s32[4]{0:T(128)S(1)}, s32[4]{0:T(128)}, u32[]{:S(2)}) copy-start(s32[4]{0:T(128)} %param.19) | copy-start | bytes 52
  0.7 19.8 %copy-start.3 = (bf16[3,3,128,128]{3,2,1,0:T(8,128)(2,1)S(1)}, bf16[3,3,128,128]{3,2,1,0:T(8,128)(2,1)}, u32[]{:S(2)}) copy-start(bf16[3,3,128,128]{3,2,1,0:T(8,128)(2,1)} %param.11) | copy-start | bytes 884740
  0.7 19.8 %copy-start.2 = (bf16[3,3,128,128]{3,2,1,0:T(8,128)(2,1)S(1)}, bf16[3,3,128,128]{3,2,1,0:T(8,128)(2,1)}, u32[]{:S(2)}) copy-start(bf16[3,3,128,128]{3,2,1,0:T(8,128)(2,1)} %param.13) | copy-start | bytes 884740
  1.9 31.1 %collective-permute-start = (bf16[64,1,256]{2,0,1:T(8,128)(2,1)S(1)}, bf16[64,1,256]{2,0,1:T(8,128)(2,1)S(1)}, u32[]{:S(2)}, u32[]{:S(2)}) collective-permute-start(bf16[64,1,256]{2,0,1:T(8,128)(2,1)S(1)} %copy.206), channel_id=1, source_target_pairs={{0,4},{4,8},{8,12},{12,0},{1,5},{5,9},{9,13},{13,1},{2,6},{6,10},{... | collective-permute-start | bytes 98312 | tf_op jit(solution)/shard_map/ppermute | solution.py:45
  5.0 28.1 %collective-permute-start.1 = (bf16[64,1,256]{2,0,1:T(8,128)(2,1)S(1)}, bf16[64,1,256]{2,0,1:T(8,128)(2,1)S(1)}, u32[]{:S(2)}, u32[]{:S(2)}) collective-permute-start(bf16[64,1,256]{2,0,1:T(8,128)(2,1)S(1)} %copy.207), channel_id=1, source_target_pairs={{4,0},{8,4},{12,8},{0,12},{5,1},{9,5},{13,9},{1,13},{6,2},{10,6},{... | collective-permute-start | bytes 98312 | tf_op jit(solution)/shard_map/ppermute | solution.py:46
  11.4 14.2 %collective-permute-start.8 = (s32[1,2]{1,0:T(1,128)S(1)}, s32[1,2]{1,0:T(1,128)S(1)}, u32[]{:S(2)}, u32[]{:S(2)}) collective-permute-start(s32[1,2]{1,0:T(1,128)S(1)} %get-tuple-element.123), channel_id=1, source_target_pairs={{0,4},{4,0},{8,12},{12,8},{1,5},{5,1},{9,13},{13,9},{2,6},{6,2},{1... | collective-permute-start | bytes 32 | tf_op jit(solution)/shard_map/ppermute | solution.py:33
  11.5 14.1 %collective-permute-start.9 = (s32[1,2]{1,0:T(1,128)S(1)}, s32[1,2]{1,0:T(1,128)S(1)}, u32[]{:S(2)}, u32[]{:S(2)}) collective-permute-start(s32[1,2]{1,0:T(1,128)S(1)} %get-tuple-element.122), channel_id=1, source_target_pairs={{0,8},{4,12},{8,0},{12,4},{1,9},{5,13},{9,1},{13,5},{2,10},{6,14},... | collective-permute-start | bytes 32 | tf_op jit(solution)/shard_map/ppermute | solution.py:33
  14.0 11.6 %collective-permute-start.10 = (s32[1,2]{1,0:T(1,128)S(1)}, s32[1,2]{1,0:T(1,128)S(1)}, u32[]{:S(2)}, u32[]{:S(2)}) collective-permute-start(s32[1,2]{1,0:T(1,128)S(1)} %get-tuple-element.121), channel_id=1, source_target_pairs={{0,12},{4,8},{8,4},{12,0},{1,13},{5,9},{9,5},{13,1},{2,14},{6,10},... | collective-permute-start | bytes 32 | tf_op jit(solution)/shard_map/ppermute | solution.py:33
  17.2 9.2 %all-to-all-start = ((s32[4,1,2]{2,1,0:T(1,128)}), s32[4,1,2]{2,1,0:T(1,128)S(1)}, u32[]{:S(2)}, u32[]{:S(2)}) async-start(s32[4,1,2]{2,1,0:T(1,128)} %bitcast.23), calls=%async_computation | async-start | bytes 4096 | tf_op jit(solution)/shard_map/all_to_all | solution.py:158
  20.5 0.7 copy-start.9
  20.8 1.5 %copy-start.6 = (bf16[4,64,128]{2,1,0:T(8,128)(2,1)S(1)}, bf16[4,64,128]{2,1,0:T(8,128)(2,1)}, u32[]{:S(2)}) copy-start(bf16[4,64,128]{2,1,0:T(8,128)(2,1)} %param.15) | copy-start | bytes 196612
  20.8 2.7 %copy-start.5 = (bf16[4,128]{1,0:T(4,128)(2,1)S(1)}, bf16[4,128]{1,0:T(4,128)(2,1)}, u32[]{:S(2)}) copy-start(bf16[4,128]{1,0:T(4,128)(2,1)} %param.16) | copy-start | bytes 3076
  21.5 11.3 %copy-start.8 = (s32[2]{0:T(128)S(1)}, s32[2]{0:T(128)}, u32[]{:S(2)}) copy-start(s32[2]{0:T(128)} %constant.69) | copy-start | bytes 28
  21.5 11.4 %copy-start.7 = (s32[2]{0:T(128)S(1)}, s32[2]{0:T(128)}, u32[]{:S(2)}) copy-start(s32[2]{0:T(128)} %constant.17) | copy-start | bytes 28
  21.6 11.4 %copy-start.4 = (bf16[64,8,256]{2,1,0:T(8,128)(2,1)S(1)}, bf16[64,8,256]{2,1,0:T(8,128)(2,1)}, u32[]{:S(2)}) copy-start(bf16[64,8,256]{2,1,0:T(8,128)(2,1)} %param.10) | copy-start | bytes 786436
  26.4 29.1 %all-to-all-start.3 = ((bf16[4,2,128]{2,1,0:T(2,128)(2,1)}), bf16[4,2,128]{2,1,0:T(2,128)(2,1)S(1)}, u32[]{:S(2)}, u32[]{:S(2)}) async-start(bf16[4,2,128]{2,1,0:T(2,128)(2,1)} %broadcast_select_fusion.2), calls=%async_computation.3 | async-start | bytes 4096 | tf_op jit(solution)/shard_map/all_to_all | solution.py:156
  33.2 6.1 %collective-permute-start.2 = (bf16[64,10,1]{2,0,1:T(8,128)(2,1)S(1)}, bf16[64,10,1]{2,0,1:T(8,128)(2,1)S(1)}, u32[]{:S(2)}, u32[]{:S(2)}) collective-permute-start(bf16[64,10,1]{2,0,1:T(8,128)(2,1)S(1)} %get-tuple-element.98), channel_id=1, source_target_pairs={{0,2},{2,0},{1,3},{3,1},{4,6},{6,4},{5,7},{7,5},{8,10},{10,8},{9,1... | collective-permute-start | bytes 3848 | tf_op jit(solution)/shard_map/ppermute | solution.py:45
  34.9 6.1 %collective-permute-start.3 = (bf16[64,10,1]{2,0,1:T(8,128)(2,1)S(1)}, bf16[64,10,1]{2,0,1:T(8,128)(2,1)S(1)}, u32[]{:S(2)}, u32[]{:S(2)}) collective-permute-start(bf16[64,10,1]{2,0,1:T(8,128)(2,1)S(1)} %get-tuple-element.99), channel_id=1, source_target_pairs={{2,0},{0,2},{3,1},{1,3},{6,4},{4,6},{7,5},{5,7},{10,8},{8,10},{11,... | collective-permute-start | bytes 3848 | tf_op jit(solution)/shard_map/ppermute | solution.py:46
  47.1 5.8 %collective-permute-start.4 = (bf16[64,1,256]{2,0,1:T(8,128)(2,1)S(1)}, bf16[64,1,256]{2,0,1:T(8,128)(2,1)S(1)}, u32[]{:S(2)}, u32[]{:S(2)}) collective-permute-start(bf16[64,1,256]{2,0,1:T(8,128)(2,1)S(1)} %get-tuple-element.116), channel_id=1, source_target_pairs={{0,4},{4,8},{8,12},{12,0},{1,5},{5,9},{9,13},{13,1},{2,6},{6,10},{... | collective-permute-start | bytes 98312 | tf_op jit(solution)/shard_map/ppermute | solution.py:45
  48.8 4.3 %collective-permute-start.5 = (bf16[64,1,256]{2,0,1:T(8,128)(2,1)S(1)}, bf16[64,1,256]{2,0,1:T(8,128)(2,1)S(1)}, u32[]{:S(2)}, u32[]{:S(2)}) collective-permute-start(bf16[64,1,256]{2,0,1:T(8,128)(2,1)S(1)} %get-tuple-element.117), channel_id=1, source_target_pairs={{4,0},{8,4},{12,8},{0,12},{5,1},{9,5},{13,9},{1,13},{6,2},{10,6},{... | collective-permute-start | bytes 98312 | tf_op jit(solution)/shard_map/ppermute | solution.py:46
  53.3 7.0 %collective-permute-start.6 = (bf16[64,10,1]{2,0,1:T(8,128)(2,1)S(1)}, bf16[64,10,1]{2,0,1:T(8,128)(2,1)S(1)}, u32[]{:S(2)}, u32[]{:S(2)}) collective-permute-start(bf16[64,10,1]{2,0,1:T(8,128)(2,1)S(1)} %get-tuple-element.96), channel_id=1, source_target_pairs={{0,2},{2,0},{1,3},{3,1},{4,6},{6,4},{5,7},{7,5},{8,10},{10,8},{9,1... | collective-permute-start | bytes 3848 | tf_op jit(solution)/shard_map/ppermute | solution.py:45
  54.8 6.8 %collective-permute-start.7 = (bf16[64,10,1]{2,0,1:T(8,128)(2,1)S(1)}, bf16[64,10,1]{2,0,1:T(8,128)(2,1)S(1)}, u32[]{:S(2)}, u32[]{:S(2)}) collective-permute-start(bf16[64,10,1]{2,0,1:T(8,128)(2,1)S(1)} %get-tuple-element.97), channel_id=1, source_target_pairs={{2,0},{0,2},{3,1},{1,3},{6,4},{4,6},{7,5},{5,7},{10,8},{8,10},{11,... | collective-permute-start | bytes 3848 | tf_op jit(solution)/shard_map/ppermute | solution.py:46
  55.5 11.5 %all-to-all-start.2 = ((bf16[4,2,64,128]{3,2,1,0:T(8,128)(2,1)}), bf16[4,2,64,128]{3,2,1,0:T(8,128)(2,1)S(1)}, u32[]{:S(2)}, u32[]{:S(2)}) async-start(bf16[4,2,64,128]{3,2,1,0:T(8,128)(2,1)} %bitcast.27), calls=%async_computation.2 | async-start | bytes 262144 | tf_op jit(solution)/shard_map/all_to_all | solution.py:155
  66.9 23.1 %all-to-all-start.1 = ((bf16[4,2,128,128]{3,2,1,0:T(8,128)(2,1)}), bf16[4,2,128,128]{3,2,1,0:T(8,128)(2,1)S(1)}, u32[]{:S(2)}, u32[]{:S(2)}) async-start(bf16[4,2,128,128]{3,2,1,0:T(8,128)(2,1)} %broadcast_select_fusion), calls=%async_computation.1 | async-start | bytes 524288 | tf_op jit(solution)/shard_map/all_to_all | solution.py:154
  97.9 5.8 %collective-permute-start.11 = (bf16[64,1,256]{2,0,1:T(8,128)(2,1)S(1)}, bf16[64,1,256]{2,0,1:T(8,128)(2,1)S(1)}, u32[]{:S(2)}, u32[]{:S(2)}) collective-permute-start(bf16[64,1,256]{2,0,1:T(8,128)(2,1)S(1)} %get-tuple-element.114), channel_id=1, source_target_pairs={{0,4},{4,8},{8,12},{12,0},{1,5},{5,9},{9,13},{13,1},{2,6},{6,10},{... | collective-permute-start | bytes 98312 | tf_op jit(solution)/shard_map/ppermute | solution.py:45
  100.0 4.0 %collective-permute-start.12 = (bf16[64,1,256]{2,0,1:T(8,128)(2,1)S(1)}, bf16[64,1,256]{2,0,1:T(8,128)(2,1)S(1)}, u32[]{:S(2)}, u32[]{:S(2)}) collective-permute-start(bf16[64,1,256]{2,0,1:T(8,128)(2,1)S(1)} %get-tuple-element.115), channel_id=1, source_target_pairs={{4,0},{8,4},{12,8},{0,12},{5,1},{9,5},{13,9},{1,13},{6,2},{10,6},{... | collective-permute-start | bytes 98312 | tf_op jit(solution)/shard_map/ppermute | solution.py:46
  104.2 6.3 %collective-permute-start.13 = (bf16[64,10,1]{2,0,1:T(8,128)(2,1)S(1)}, bf16[64,10,1]{2,0,1:T(8,128)(2,1)S(1)}, u32[]{:S(2)}, u32[]{:S(2)}) collective-permute-start(bf16[64,10,1]{2,0,1:T(8,128)(2,1)S(1)} %get-tuple-element.94), channel_id=1, source_target_pairs={{0,2},{2,0},{1,3},{3,1},{4,6},{6,4},{5,7},{7,5},{8,10},{10,8},{9,1... | collective-permute-start | bytes 3848 | tf_op jit(solution)/shard_map/ppermute | solution.py:45
  105.7 6.5 %collective-permute-start.14 = (bf16[64,10,1]{2,0,1:T(8,128)(2,1)S(1)}, bf16[64,10,1]{2,0,1:T(8,128)(2,1)S(1)}, u32[]{:S(2)}, u32[]{:S(2)}) collective-permute-start(bf16[64,10,1]{2,0,1:T(8,128)(2,1)S(1)} %get-tuple-element.95), channel_id=1, source_target_pairs={{2,0},{0,2},{3,1},{1,3},{6,4},{4,6},{7,5},{5,7},{10,8},{8,10},{11,... | collective-permute-start | bytes 3848 | tf_op jit(solution)/shard_map/ppermute | solution.py:46
  116.7 1.0 copy-start.10
  118.3 5.8 %collective-permute-start.15 = (bf16[64,1,256]{2,0,1:T(8,128)(2,1)S(1)}, bf16[64,1,256]{2,0,1:T(8,128)(2,1)S(1)}, u32[]{:S(2)}, u32[]{:S(2)}) collective-permute-start(bf16[64,1,256]{2,0,1:T(8,128)(2,1)S(1)} %get-tuple-element.112), channel_id=1, source_target_pairs={{0,4},{4,8},{8,12},{12,0},{1,5},{5,9},{9,13},{13,1},{2,6},{6,10},{... | collective-permute-start | bytes 98312 | tf_op jit(solution)/shard_map/ppermute | solution.py:45
  119.7 4.4 %collective-permute-start.16 = (bf16[64,1,256]{2,0,1:T(8,128)(2,1)S(1)}, bf16[64,1,256]{2,0,1:T(8,128)(2,1)S(1)}, u32[]{:S(2)}, u32[]{:S(2)}) collective-permute-start(bf16[64,1,256]{2,0,1:T(8,128)(2,1)S(1)} %get-tuple-element.113), channel_id=1, source_target_pairs={{4,0},{8,4},{12,8},{0,12},{5,1},{9,5},{13,9},{1,13},{6,2},{10,6},{... | collective-permute-start | bytes 98312 | tf_op jit(solution)/shard_map/ppermute | solution.py:46
  124.3 7.1 %collective-permute-start.17 = (bf16[64,10,1]{2,0,1:T(8,128)(2,1)S(1)}, bf16[64,10,1]{2,0,1:T(8,128)(2,1)S(1)}, u32[]{:S(2)}, u32[]{:S(2)}) collective-permute-start(bf16[64,10,1]{2,0,1:T(8,128)(2,1)S(1)} %get-tuple-element.92), channel_id=1, source_target_pairs={{0,2},{2,0},{1,3},{3,1},{4,6},{6,4},{5,7},{7,5},{8,10},{10,8},{9,1... | collective-permute-start | bytes 3848 | tf_op jit(solution)/shard_map/ppermute | solution.py:45
  125.8 7.3 %collective-permute-start.18 = (bf16[64,10,1]{2,0,1:T(8,128)(2,1)S(1)}, bf16[64,10,1]{2,0,1:T(8,128)(2,1)S(1)}, u32[]{:S(2)}, u32[]{:S(2)}) collective-permute-start(bf16[64,10,1]{2,0,1:T(8,128)(2,1)S(1)} %get-tuple-element.93), channel_id=1, source_target_pairs={{2,0},{0,2},{3,1},{1,3},{6,4},{4,6},{7,5},{5,7},{10,8},{8,10},{11,... | collective-permute-start | bytes 3848 | tf_op jit(solution)/shard_map/ppermute | solution.py:46
  126.4 13.2 %all-to-all-start.4 = ((bf16[4,2,64,128]{3,2,1,0:T(8,128)(2,1)}), bf16[4,2,64,128]{3,2,1,0:T(8,128)(2,1)S(1)}, u32[]{:S(2)}, u32[]{:S(2)}) async-start(bf16[4,2,64,128]{3,2,1,0:T(8,128)(2,1)} %bitcast.61), calls=%async_computation.4 | async-start | bytes 262144 | tf_op jit(solution)/shard_map/all_to_all | solution.py:169
